TPU v7x, 256 devices: a whole 4x4x8 slice. The times are simulated.
256 devices in a mesh: tm: 64 (over z, x, core), blk: 4 (over y).
Axes of the slice: x: 4, y: 4, z: 8, core: 2. Of those that a mesh axis runs over, the one named last changes fastest.
Arguments:
- prior_mean: float32 [512], replicated, may hold values from -6 to 6
- after_mean: float32 [512], replicated, may hold values from -6 to 6
- filter_map: float32 [128, 512, 512], P('tm', 'blk'), may hold values from -1 to 1.5
- smoother_gain: float32 [128, 512, 512], P('tm', 'blk'), may hold values from -1 to 1.5
- smoother_map: float32 [128, 512, 512], P('tm', 'blk'), may hold values from -1 to 1.5
- obs_gain: float32 [128, 512, 128], P('tm', 'blk'), may hold values from -0.5 to 0.5
- observations: float32 [128, 128], P('tm'), may hold values from -6 to 6
Outputs:
- filtered: float32 [128, 512], P('tm', 'blk')
- smoothed: float32 [128, 512], P('tm', 'blk')
All inputs are finite; a program needn't handle non-finite values.
Results may differ from a plain program's by a relative error of at most 0.0003.
Values sent between devices are 32-bit elements; how exact they have to be, the bound alone decides.
A program may use at most 128 MiB of HBM per device.

v0:
```python
import jax
import jax.numpy as jnp
from jax import lax
from jax.sharding import Mesh
from jax.sharding import PartitionSpec as P

TM = ("tm_0", "tm_1", "tm_2")


def neutral_like(value, identity):
    return jax.tree.map(
        lambda part, zero: jnp.zeros_like(part) + jnp.asarray(zero, part.dtype), value, identity
    )


def prefix_by_axis(value, axes, combine, identity, reverse):
    before = start = neutral_like(value, identity)
    so_far = value
    for axis in reversed(axes):
        length, index = (lax.axis_size(axis), lax.axis_index(axis))
        pieces = jax.tree.map(lambda part: lax.all_gather(part, axis), so_far)
        inside, so_far = (start, start)
        for k in reversed(range(length)) if reverse else range(length):
            passed = k > index if reverse else k < index
            so_far = combine(so_far, jax.tree.map(lambda part: part[k], pieces))
            inside = jax.tree.map(lambda new, old: jnp.where(passed, new, old), so_far, inside)
        before = combine(inside, before)
    return before


def chain_combine(earlier, later):
    highest = lax.Precision.HIGHEST
    joined_map = jnp.dot(later[0], earlier[0], precision=highest)
    joined_offset = jnp.dot(later[0], earlier[1], precision=highest) + later[1]
    return (joined_map, joined_offset)


def shards(prior_mean, after_mean, filter_map, smoother_gain, smoother_map, obs_gain, observations):
    highest = lax.Precision.HIGHEST
    steps = filter_map.shape[0]
    rows = filter_map.shape[1]
    width = filter_map.shape[2]
    first_row = lax.axis_index("blk") * rows
    drive_rows = jnp.einsum("tro,to->tr", obs_gain, observations, precision=highest)
    full_filter, full_gain, drive = (
        lax.all_gather(filter_map, "blk", axis=1, tiled=True),
        lax.all_gather(smoother_gain, "blk", axis=1, tiled=True),
        lax.all_gather(drive_rows, "blk", axis=1, tiled=True),
    )
    identity = jnp.eye(width, dtype=jnp.float32)
    nothing = jnp.zeros((width,), jnp.float32)
    offset = nothing
    for index in range(steps):
        offset = jnp.dot(full_filter[index], offset, precision=highest) + drive[index]
    composite = full_filter[steps - 1]
    index = 0
    composite = jnp.dot(composite, full_filter[index], precision=highest)
    total = prefix_by_axis((composite, offset), TM, chain_combine, (identity, nothing), False)
    entering = jnp.dot(total[0], prior_mean, precision=highest) + total[1]
    current = entering
    filtered_list = []
    for index in range(steps):
        current = jnp.dot(full_filter[index], current, precision=highest) + drive[index]
        filtered_list.append(current)
    filtered_full = jnp.stack(filtered_list, axis=0)
    filtered_rows = lax.dynamic_slice_in_dim(filtered_full, first_row, rows, 1)
    pulled_rows = jnp.einsum("trk,tk->tr", smoother_map, filtered_full, precision=highest)
    pulled = lax.all_gather(pulled_rows, "blk", axis=1, tiled=True)
    offset = nothing
    for index in range(steps - 1, -1, -1):
        offset = jnp.dot(full_gain[index], offset, precision=highest) + pulled[index]
    composite = full_gain[0]
    index = 1
    composite = jnp.dot(composite, full_gain[index], precision=highest)
    total = prefix_by_axis((composite, offset), TM, chain_combine, (identity, nothing), True)
    leaving = jnp.dot(total[0], after_mean, precision=highest) + total[1]
    current = leaving
    smoothed_list = []
    for index in range(steps - 1, -1, -1):
        current = jnp.dot(full_gain[index], current, precision=highest) + pulled[index]
        smoothed_list.append(current)
    smoothed_full = jnp.stack(smoothed_list[::-1], axis=0)
    smoothed_rows = lax.dynamic_slice_in_dim(smoothed_full, first_row, rows, 1)
    return (filtered_rows, smoothed_rows)


def solution(mesh):
    torus = Mesh(mesh.devices.reshape(8, 4, 2, mesh.shape["blk"]), ("tm_0", "tm_1", "tm_2", "blk"))
    in_specs = (
        P(),
        P(),
        P(TM, "blk", None),
        P(TM, "blk", None),
        P(TM, "blk", None),
        P(TM, "blk", None),
        P(TM, None),
    )
    out_specs = (P(TM, "blk"), P(TM, "blk"))
    return jax.shard_map(
        shards, mesh=torus, in_specs=in_specs, out_specs=out_specs, check_vma=False
    )
```

profile of v0, /device:TPU:1, one launch (start us, length us, event | category | flops | bytes accessed | tf_op | source)
XLA Modules:
  0.0 462.8 jit_solution(7283257458123513231)
XLA Ops:
  8.7 38.1 %all-gather.27.cloned.1.call-done = f32[2,512,512]{2,1,0:T(8,128)} async-done(((f32[2,128,512]{2,1,0:T(8,128)}), f32[2,512,512]{2,1,0:T(8,128)}) %all-gather.27.cloned.1.call-update) | async-done | bytes 2097168 | tf_op jit(solution)/shard_map/all_gather | solution.py:46
  46.8 4.4 fusion.142
  51.2 30.8 %all-gather.29.cloned.1.call-done = f32[2,512,512]{2,1,0:T(8,128)} async-done(((f32[2,128,512]{2,1,0:T(8,128)}), f32[2,512,512]{2,1,0:T(8,128)}) %all-gather.29.cloned.1.call-update) | async-done | bytes 2097168 | tf_op jit(solution)/shard_map/all_gather | solution.py:47
  82.0 4.4 fusion.147
  86.5 14.2 %all-gather.31.cloned.1.call-done = f32[1024,512]{1,0:T(8,128)} async-done(((f32[512,512]{1,0:T(8,128)}), f32[1024,512]{1,0:T(8,128)}) %all-gather.31.cloned.1.call-update) | async-done | bytes 2097168 | tf_op jit(solution)/shard_map/all_gather | solution.py:21
  100.7 2.2 fusion.35
  102.9 4.4 fusion.136
  107.4 12.2 %all-gather.37.cloned.1.call-done = f32[1024,512]{1,0:T(8,128)} async-done(((f32[512,512]{1,0:T(8,128)}), f32[1024,512]{1,0:T(8,128)}) %all-gather.37.cloned.1.call-update) | async-done | bytes 2097168 | tf_op jit(solution)/shard_map/all_gather | solution.py:21
  119.6 2.2 fusion.31
  121.8 4.4 fusion.84
  126.4 46.0 %all-gather.33.cloned.1.call-done = f32[2048,512]{1,0:T(8,128)} async-done(((f32[512,512]{1,0:T(8,128)}), f32[2048,512]{1,0:T(8,128)}) %all-gather.33.cloned.1.call-update) | async-done | bytes 4194320 | tf_op jit(solution)/shard_map/all_gather | solution.py:21
  172.4 2.3 fusion.34
  175.8 3.1 fusion.121
  182.7 2.8 fusion.129
  186.0 8.1 %all_gather.91 = f32[2,512]{1,0:T(2,128)S(1)} all-gather(f32[2,128]{1,0:T(2,128)S(1)} %bitcast.347), channel_id=1, replica_groups=mesh['tm_0'=8,'tm_1'=4,'tm_2'=2,'blk'=4] {'blk'}, dimensions={1}, use_global_device_ids=true | all-gather | bytes 5120 | tf_op jit(solution)/shard_map/all_gather | solution.py:48
  194.1 2.2 fusion.144
  196.3 2.2 fusion.141
  198.5 4.2 all-gather.12
  203.6 21.6 %all-gather.39.cloned.1.call-done = f32[2048,512]{1,0:T(8,128)} async-done(((f32[512,512]{1,0:T(8,128)}), f32[2048,512]{1,0:T(8,128)}) %all-gather.39.cloned.1.call-update) | async-done | bytes 4194320 | tf_op jit(solution)/shard_map/all_gather | solution.py:21
  225.2 2.3 fusion.30
  228.5 3.1 fusion.69
  235.5 2.8 fusion.77
  238.4 2.5 fusion.134
  240.9 2.3 fusion.138
  243.2 9.4 %all-gather.13 = f32[4,1,512]{2,1,0:T(1,128)S(1)} all-gather(f32[1,1,512]{2,1,0:T(1,128)S(1)} %bitcast.331), channel_id=6, replica_groups=mesh['tm_0'=8,'tm_1'=4,'tm_2'=2,'blk'=4] {'tm_1'}, dimensions={0}, use_global_device_ids=true | all-gather | bytes 10240 | tf_op jit(solution)/shard_map/all_gather | solution.py:21
  253.0 2.2 fusion.82
  261.7 22.3 %all-gather.14 = f32[8,1,512]{2,1,0:T(1,128)S(1)} all-gather(f32[1,1,512]{2,1,0:T(1,128)S(1)} %bitcast.342), channel_id=7, replica_groups=mesh['tm_0'=8,'tm_1'=4,'tm_2'=2,'blk'=4] {'tm_0'}, dimensions={0}, use_global_device_ids=true | all-gather | bytes 18432 | tf_op jit(solution)/shard_map/all_gather | solution.py:21
  284.0 2.4 fusion.67
  287.4 3.0 fusion.6
  290.4 3.0 fusion.20
  293.4 28.4 %all-gather.35.cloned.1.call-done = f32[4096,512]{1,0:T(8,128)} async-done(((f32[512,512]{1,0:T(8,128)}), f32[4096,512]{1,0:T(8,128)}) %all-gather.35.cloned.1.call-update) | async-done | bytes 8388624 | tf_op jit(solution)/shard_map/all_gather | solution.py:21
  321.8 2.3 fusion.89
  324.1 2.3 fusion.93
  326.5 2.5 fusion.97
  329.0 2.2 fusion.101
  331.2 2.2 fusion.105
  333.4 2.3 fusion.109
  335.8 2.2 fusion.113
  338.0 2.2 fusion.116
  342.4 1.9 fusion.91
  344.3 1.9 fusion.95
  346.1 1.9 fusion.99
  348.0 1.9 fusion.103
  349.9 1.9 fusion.107
  351.7 1.9 fusion.111
  353.6 2.3 convolution_select_fusion.1
  361.3 8.5 %all_gather.105 = f32[2,512]{1,0:T(2,128)S(1)} all-gather(f32[2,128]{1,0:T(2,128)S(1)} %bitcast.346), channel_id=1, replica_groups=mesh['tm_0'=8,'tm_1'=4,'tm_2'=2,'blk'=4] {'blk'}, dimensions={1}, use_global_device_ids=true | all-gather | bytes 5120 | tf_op jit(solution)/shard_map/all_gather | solution.py:68
  370.8 3.6 all-gather.15
  375.4 9.5 %all-gather.16 = f32[4,1,512]{2,1,0:T(1,128)S(1)} all-gather(f32[1,1,512]{2,1,0:T(1,128)S(1)} %bitcast.330), channel_id=12, replica_groups=mesh['tm_0'=8,'tm_1'=4,'tm_2'=2,'blk'=4] {'tm_1'}, dimensions={0}, use_global_device_ids=true | all-gather | bytes 10240 | tf_op jit(solution)/shard_map/all_gather | solution.py:21
  387.9 19.5 %all-gather.17 = f32[8,1,512]{2,1,0:T(1,128)S(1)} all-gather(f32[1,1,512]{2,1,0:T(1,128)S(1)} %bitcast.339), channel_id=13, replica_groups=mesh['tm_0'=8,'tm_1'=4,'tm_2'=2,'blk'=4] {'tm_0'}, dimensions={0}, use_global_device_ids=true | all-gather | bytes 18432 | tf_op jit(solution)/shard_map/all_gather | solution.py:21
  408.7 7.8 %all-gather.41.cloned.1.call-done = f32[4096,512]{1,0:T(8,128)} async-done(((f32[512,512]{1,0:T(8,128)}), f32[4096,512]{1,0:T(8,128)}) %all-gather.41.cloned.1.call-update) | async-done | bytes 8388624 | tf_op jit(solution)/shard_map/all_gather | solution.py:21
  416.5 2.3 fusion.37
  418.8 2.3 fusion.41
  421.2 2.5 fusion.45
  423.7 2.2 fusion.49
  426.0 2.2 fusion.53
  428.2 2.2 fusion.57
  430.4 2.2 fusion.61
  432.6 2.2 fusion.64
  438.7 1.9 fusion.43
  440.6 2.0 fusion.47
  444.5 1.9 fusion.55
  446.3 1.9 fusion.59
  448.2 2.1 convolution_select_fusion
  (174 shorter events, 45.8 us)
Async XLA Ops:
  7.2 353.7 %copy-start = (f32[2,128,512]{2,1,0:T(8,128)S(1)}, f32[2,128,512]{2,1,0:T(8,128)}, u32[]{:S(2)}) copy-start(f32[2,128,512]{2,1,0:T(8,128)} %param.11) | copy-start | bytes 1572868
  7.2 39.6 %all-gather.27.cloned.1.call-start = ((), (), s32[]{:S(2)}) async-start(), calls=%async_computation | async-start | bytes 2621440 | tf_op jit(solution)/shard_map/all_gather | solution.py:46
  7.9 74.1 %all-gather.29.cloned.1.call-start = ((), (), s32[]{:S(2)}) async-start(), calls=%async_computation.1 | async-start | bytes 2621440 | tf_op jit(solution)/shard_map/all_gather | solution.py:47
  8.7 92.0 %all-gather.31.cloned.1.call-start = ((), (), s32[]{:S(2)}) async-start(), calls=%async_computation.2 | async-start | bytes 3145728 | tf_op jit(solution)/shard_map/all_gather | solution.py:21
  51.2 68.4 %all-gather.37.cloned.1.call-start = ((), (), s32[]{:S(2)}) async-start(), calls=%async_computation.5 | async-start | bytes 3145728 | tf_op jit(solution)/shard_map/all_gather | solution.py:21
  86.4 86.0 %all-gather.33.cloned.1.call-start = ((), (), s32[]{:S(2)}) async-start(), calls=%async_computation.3 | async-start | bytes 5242880 | tf_op jit(solution)/shard_map/all_gather | solution.py:21
  102.9 23.3 %copy-start.13 = (f32[512,512]{1,0:T(8,128)}, f32[512,512]{1,0:T(8,128)S(1)}, u32[]{:S(2)}) copy-start(f32[512,512]{1,0:T(8,128)S(1)} %fusion.35) | copy-start | bytes 3145732
  107.3 117.9 %all-gather.39.cloned.1.call-start = ((), (), s32[]{:S(2)}) async-start(), calls=%async_computation.6 | async-start | bytes 5242880 | tf_op jit(solution)/shard_map/all_gather | solution.py:21
  121.8 53.0 %copy-start.16 = (f32[512,512]{1,0:T(8,128)}, f32[512,512]{1,0:T(8,128)S(1)}, u32[]{:S(2)}) copy-start(f32[512,512]{1,0:T(8,128)S(1)} %fusion.31) | copy-start | bytes 3145732
  126.2 195.6 %all-gather.35.cloned.1.call-start = ((), (), s32[]{:S(2)}) async-start(), calls=%async_computation.4 | async-start | bytes 9437184 | tf_op jit(solution)/shard_map/all_gather | solution.py:21
  172.4 7.4 %copy-start.7 = (f32[2048,512]{1,0:T(8,128)S(1)}, f32[2048,512]{1,0:T(8,128)}, u32[]{:S(2)}) copy-start(f32[2048,512]{1,0:T(8,128)} %all-gather.33.cloned.1.call-done) | copy-start | bytes 12582916
  174.8 1.0 copy-start.26
  178.8 1.0 copy-start.9
  179.8 5.8 %copy-start.34 = (f32[2,128,128]{2,1,0:T(8,128)S(1)}, f32[2,128,128]{2,1,0:T(8,128)}, u32[]{:S(2)}) copy-start(f32[2,128,128]{2,1,0:T(8,128)} %param.12) | copy-start | bytes 393220
  179.8 5.8 %copy-start.37 = (f32[2,128]{1,0:T(2,128)S(1)}, f32[2,128]{1,0:T(2,128)}, u32[]{:S(2)}) copy-start(f32[2,128]{1,0:T(2,128)} %param.13) | copy-start | bytes 3076
  179.8 22.9 %copy-start.3 = (f32[2,512,512]{2,1,0:T(8,128)S(1)}, f32[2,512,512]{2,1,0:T(8,128)}, u32[]{:S(2)}) copy-start(f32[2,512,512]{2,1,0:T(8,128)} %all-gather.29.cloned.1.call-done) | copy-start | bytes 6291460
  181.7 1.0 copy-start.11
  185.6 231.0 %all-gather.41.cloned.1.call-start = ((), (), s32[]{:S(2)}) async-start(), calls=%async_computation.7 | async-start | bytes 9437184 | tf_op jit(solution)/shard_map/all_gather | solution.py:21
  225.2 7.4 %copy-start.5 = (f32[2048,512]{1,0:T(8,128)S(1)}, f32[2048,512]{1,0:T(8,128)}, u32[]{:S(2)}) copy-start(f32[2048,512]{1,0:T(8,128)} %all-gather.39.cloned.1.call-done) | copy-start | bytes 12582916
  227.5 1.0 copy-start.28
  231.6 1.0 copy-start.19
  234.4 1.0 copy-start.21
  238.3 16.9 %copy-start.14 = (f32[512,512]{1,0:T(8,128)S(1)}, f32[512,512]{1,0:T(8,128)}, u32[]{:S(2)}) copy-start(f32[512,512]{1,0:T(8,128)} %copy-done.13) | copy-start | bytes 3145732
  238.3 16.9 %copy-start.15 = (f32[512,512]{1,0:T(8,128)S(1)}, f32[512,512]{1,0:T(8,128)}, u32[]{:S(2)}) copy-start(f32[512,512]{1,0:T(8,128)} %fusion.136) | copy-start | bytes 3145732
  238.3 18.1 %copy-start.17 = (f32[512,512]{1,0:T(8,128)S(1)}, f32[512,512]{1,0:T(8,128)}, u32[]{:S(2)}) copy-start(f32[512,512]{1,0:T(8,128)} %copy-done.16) | copy-start | bytes 3145732
  238.3 18.1 %copy-start.18 = (f32[512,512]{1,0:T(8,128)S(1)}, f32[512,512]{1,0:T(8,128)}, u32[]{:S(2)}) copy-start(f32[512,512]{1,0:T(8,128)} %fusion.84) | copy-start | bytes 3145732
  240.8 16.8 %copy-start.8 = (f32[2048,512]{1,0:T(8,128)S(1)}, f32[2048,512]{1,0:T(8,128)}, u32[]{:S(2)}) copy-start(f32[2048,512]{1,0:T(8,128)} %all-gather.33.cloned.1.call-done) | copy-start | bytes 12582916
  256.4 31.0 %copy-start.10 = (f32[512,512]{1,0:T(8,128)S(1)}, f32[512,512]{1,0:T(8,128)}, u32[]{:S(2)}) copy-start(f32[512,512]{1,0:T(8,128)} %copy-done.9) | copy-start | bytes 3145732
  256.4 31.0 %copy-start.12 = (f32[512,512]{1,0:T(8,128)S(1)}, f32[512,512]{1,0:T(8,128)}, u32[]{:S(2)}) copy-start(f32[512,512]{1,0:T(8,128)} %copy-done.11) | copy-start | bytes 3145732
  256.4 31.0 %copy-start.25 = (f32[512,512]{1,0:T(8,128)S(1)}, f32[512,512]{1,0:T(8,128)}, u32[]{:S(2)}) copy-start(f32[512,512]{1,0:T(8,128)} %fusion.129) | copy-start | bytes 3145732
  256.4 31.0 %copy-start.27 = (f32[512,512]{1,0:T(8,128)S(1)}, f32[512,512]{1,0:T(8,128)}, u32[]{:S(2)}) copy-start(f32[512,512]{1,0:T(8,128)} %copy-done.26) | copy-start | bytes 3145732
  257.6 32.8 %copy-start.31 = (f32[512,512]{1,0:T(8,128)}, f32[512,512]{1,0:T(8,128)S(1)}, u32[]{:S(2)}) copy-start(f32[512,512]{1,0:T(8,128)S(1)} %fusion.15) | copy-start | bytes 3145732
  284.0 6.4 %copy-start.20 = (f32[512,512]{1,0:T(8,128)S(1)}, f32[512,512]{1,0:T(8,128)}, u32[]{:S(2)}) copy-start(f32[512,512]{1,0:T(8,128)} %copy-done.19) | copy-start | bytes 3145732
  284.0 6.4 %copy-start.22 = (f32[512,512]{1,0:T(8,128)S(1)}, f32[512,512]{1,0:T(8,128)}, u32[]{:S(2)}) copy-start(f32[512,512]{1,0:T(8,128)} %copy-done.21) | copy-start | bytes 3145732
  284.0 6.4 %copy-start.23 = (f32[512,512]{1,0:T(8,128)S(1)}, f32[512,512]{1,0:T(8,128)}, u32[]{:S(2)}) copy-start(f32[512,512]{1,0:T(8,128)} %fusion.77) | copy-start | bytes 3145732
  284.0 6.4 %copy-start.29 = (f32[512,512]{1,0:T(8,128)S(1)}, f32[512,512]{1,0:T(8,128)}, u32[]{:S(2)}) copy-start(f32[512,512]{1,0:T(8,128)} %copy-done.28) | copy-start | bytes 3145732
  321.8 18.5 %copy-start.30 = (f32[512,512]{1,0:T(8,128)S(1)}, f32[512,512]{1,0:T(8,128)}, u32[]{:S(2)}) copy-start(f32[512,512]{1,0:T(8,128)} %fusion.6) | copy-start | bytes 3145732
  324.1 17.1 %copy-start.2 = (f32[4096,512]{1,0:T(8,128)S(1)}, f32[4096,512]{1,0:T(8,128)}, u32[]{:S(2)}) copy-start(f32[4096,512]{1,0:T(8,128)} %all-gather.35.cloned.1.call-done) | copy-start | bytes 25165828
  353.6 4.2 copy-start.35
  353.6 20.8 %copy-start.33 = (f32[1024,512]{1,0:T(8,128)S(1)}, f32[1024,512]{1,0:T(8,128)}, u32[]{:S(2)}) copy-start(f32[1024,512]{1,0:T(8,128)} %all-gather.37.cloned.1.call-done) | copy-start | bytes 6291460
  355.9 2.9 copy-start.4
  355.9 28.9 %copy-start.6 = (f32[2048,512]{1,0:T(8,128)S(1)}, f32[2048,512]{1,0:T(8,128)}, u32[]{:S(2)}) copy-start(f32[2048,512]{1,0:T(8,128)} %all-gather.39.cloned.1.call-done) | copy-start | bytes 12582916
  358.8 48.9 %copy-start.32 = (f32[512,512]{1,0:T(8,128)S(1)}, f32[512,512]{1,0:T(8,128)}, u32[]{:S(2)}) copy-start(f32[512,512]{1,0:T(8,128)} %copy-done.31) | copy-start | bytes 3145732
  416.5 18.3 %copy-start.24 = (f32[512,512]{1,0:T(8,128)S(1)}, f32[512,512]{1,0:T(8,128)}, u32[]{:S(2)}) copy-start(f32[512,512]{1,0:T(8,128)} %fusion.20) | copy-start | bytes 3145732
  418.8 17.0 %copy-start.1 = (f32[4096,512]{1,0:T(8,128)S(1)}, f32[4096,512]{1,0:T(8,128)}, u32[]{:S(2)}) copy-start(f32[4096,512]{1,0:T(8,128)} %all-gather.41.cloned.1.call-done) | copy-start | bytes 25165828
  448.2 4.0 copy-start.36
Sparse Core Ops, SparseCore 0:
  9.8 36.9 all-gather.26
  48.6 33.3 all-gather.28
  83.8 16.8 all-gather.30
  102.3 17.1 all-gather.36
  121.2 51.1 all-gather.32
  174.1 51.0 all-gather.38
  227.0 94.7 all-gather.34
  323.6 92.9 all-gather.40
where the time goes:
time: 471 us; the launch traced here: 463 us
  waiting for transfers between devices  200 us (42%)
  matrix products  155 us (33%)
  blocking collectives  85.1 us (18%)
  between operations  15.1 us (3%)
  local copies, waits for them, and re-layouts  6.15 us (1%)
    all_gather x6, waiting for transfers between devices, prefix_by_axis(): pieces = jax.tree.map(lambda part: lax.all_gather(part, axis), so_far)  130 us
    dot_general x34, matrix products, chain_combine(): joined_map = jnp.dot(later[0], earlier[0], precision=highest)  74.4 us
    all_gather x6, blocking collectives, prefix_by_axis(): pieces = jax.tree.map(lambda part: lax.all_gather(part, axis), so_far)  68.5 us
    dot_general x34, matrix products, chain_combine(): joined_offset = jnp.dot(later[0], earlier[1], precision=highest) + later[1]  58.5 us
    all_gather x1, waiting for transfers between devices, shards(): lax.all_gather(filter_map, 'blk', axis=1, tiled=True)  38.1 us
    all_gather x1, waiting for transfers between devices, shards(): lax.all_gather(smoother_gain, 'blk', axis=1, tiled=True)  30.8 us
  transfers between devices with their start and end apart: 8, of which 8 were waited for; matrix products, arithmetic and copies ran while one was open for 25% of the time, Pallas kernels for 0%

commit v1 on v0

--- a/solution.py
+++ b/solution.py
@@ -5,6 +5,24 @@
 from jax.sharding import PartitionSpec as P
 
 TM = ("tm_0", "tm_1", "tm_2")
+
+
+def ring_gather(shard, axis, dim):
+    ways, here, step = (lax.axis_size(axis), lax.axis_index(axis), shard.shape[dim])
+    shape = [n * ways if d == dim else n for d, n in enumerate(shard.shape)]
+    full = lax.dynamic_update_slice_in_dim(
+        jnp.zeros(shape, shard.dtype), shard, here * step, axis=dim
+    )
+    going_up = going_down = shard
+    for far in range(1, ways // 2 + 1):
+        going_up = lax.ppermute(going_up, axis, [(d, (d + 1) % ways) for d in range(ways)])
+        full = lax.dynamic_update_slice_in_dim(full, going_up, (here - far) % ways * step, axis=dim)
+        if 2 * far < ways:
+            going_down = lax.ppermute(going_down, axis, [(d, (d - 1) % ways) for d in range(ways)])
+            full = lax.dynamic_update_slice_in_dim(
+                full, going_down, (here + far) % ways * step, axis=dim
+            )
+    return full
 
 
 def neutral_like(value, identity):
@@ -44,7 +62,7 @@
     drive_rows = jnp.einsum("tro,to->tr", obs_gain, observations, precision=highest)
     full_filter, full_gain, drive = (
         lax.all_gather(filter_map, "blk", axis=1, tiled=True),
-        lax.all_gather(smoother_gain, "blk", axis=1, tiled=True),
+        ring_gather(smoother_gain, "blk", 1),
         lax.all_gather(drive_rows, "blk", axis=1, tiled=True),
     )
     identity = jnp.eye(width, dtype=jnp.float32)

time: 471 us -> 514 us (1.091)
  the two profiles are of different devices: /device:TPU:1 before, /device:TPU:32 now
where the time goes in v1:
time: 514 us; the launch traced here: 506 us
  waiting for transfers between devices  229 us (45%)
  matrix products  152 us (30%)
  blocking collectives  92.1 us (18%)
  between operations  15.4 us (3%)
  local copies, waits for them, and re-layouts  11.7 us (2%)
    all_gather x6, waiting for transfers between devices, prefix_by_axis(): pieces = jax.tree.map(lambda part: lax.all_gather(part, axis), so_far)  192 us
    dot_general x34, matrix products, chain_combine(): joined_map = jnp.dot(later[0], earlier[0], precision=highest)  78.9 us
    all_gather x6, blocking collectives, prefix_by_axis(): pieces = jax.tree.map(lambda part: lax.all_gather(part, axis), so_far)  72.5 us
    dot_general x34, matrix products, chain_combine(): joined_offset = jnp.dot(later[0], earlier[1], precision=highest) + later[1]  55.5 us
    ppermute x2, waiting for transfers between devices, ring_gather(): lax.ppermute(going_up, axis, [(d, (d + 1) % ways) for d in range(ways)])  33.8 us
  transfers between devices with their start and end apart: 10, of which 9 were waited for; matrix products, arithmetic and copies ran while one was open for 18% of the time, Pallas kernels for 0%

profile of v1, /device:TPU:32, one launch (start us, length us, event | category | flops | bytes accessed | tf_op | source)
XLA Modules:
  0.0 505.6 jit_solution(1677800865238200108)
XLA Ops:
  11.3 11.9 %collective-permute-done = f32[2,128,512]{2,1,0:T(8,128)S(1)} collective-permute-done((f32[2,128,512]{2,1,0:T(8,128)}, f32[2,128,512]{2,1,0:T(8,128)S(1)}, u32[]{:S(2)}, u32[]{:S(2)}) %collective-permute-start) | collective-permute-done | bytes 524320 | tf_op jit(solution)/shard_map/ppermute | solution.py:18
  26.0 21.9 %collective-permute-done.2 = f32[2,128,512]{2,1,0:T(8,128)} collective-permute-done((f32[2,128,512]{2,1,0:T(8,128)S(1)}, f32[2,128,512]{2,1,0:T(8,128)}, u32[]{:S(2)}, u32[]{:S(2)}) %collective-permute-start.2) | collective-permute-done | bytes 524320 | tf_op jit(solution)/shard_map/ppermute | solution.py:18
  49.0 2.9 fusion.147
  52.0 2.5 all-gather.26.cloned.1.call-done
  54.5 4.4 fusion.142
  58.9 13.5 %all-gather.34.cloned.1.call-done = f32[1024,512]{1,0:T(8,128)} async-done(((f32[512,512]{1,0:T(8,128)}), f32[1024,512]{1,0:T(8,128)}) %all-gather.34.cloned.1.call-update) | async-done | bytes 2097168 | tf_op jit(solution)/shard_map/all_gather | solution.py:39
  72.4 2.2 fusion.31
  75.6 4.1 fusion.84
  79.9 11.5 %all-gather.28.cloned.1.call-done = f32[1024,512]{1,0:T(8,128)} async-done(((f32[512,512]{1,0:T(8,128)}), f32[1024,512]{1,0:T(8,128)}) %all-gather.28.cloned.1.call-update) | async-done | bytes 2097168 | tf_op jit(solution)/shard_map/all_gather | solution.py:39
  91.4 2.2 fusion.35
  94.6 4.0 fusion.136
  98.7 46.4 %all-gather.36.cloned.1.call-done = f32[2048,512]{1,0:T(8,128)} async-done(((f32[512,512]{1,0:T(8,128)}), f32[2048,512]{1,0:T(8,128)}) %all-gather.36.cloned.1.call-update) | async-done | bytes 4194320 | tf_op jit(solution)/shard_map/all_gather | solution.py:39
  145.1 2.3 fusion.30
  148.5 3.1 fusion.69
  155.4 2.8 fusion.77
  158.7 39.2 %all-gather.30.cloned.1.call-done = f32[2048,512]{1,0:T(8,128)} async-done(((f32[512,512]{1,0:T(8,128)}), f32[2048,512]{1,0:T(8,128)}) %all-gather.30.cloned.1.call-update) | async-done | bytes 4194320 | tf_op jit(solution)/shard_map/all_gather | solution.py:39
  197.9 2.3 fusion.34
  201.3 3.1 fusion.121
  208.3 2.8 fusion.129
  211.5 9.9 %all_gather.88 = f32[2,512]{1,0:T(2,128)S(1)} all-gather(f32[2,128]{1,0:T(2,128)S(1)} %bitcast.347), channel_id=1, replica_groups=mesh['tm_0'=8,'tm_1'=4,'tm_2'=2,'blk'=4] {'blk'}, dimensions={1}, use_global_device_ids=true | all-gather | bytes 5120 | tf_op jit(solution)/shard_map/all_gather | solution.py:66
  222.3 2.4 fusion.82
  224.7 2.4 fusion.15
  229.1 2.0 all-gather.12
  233.2 10.4 %all-gather.13 = f32[4,1,512]{2,1,0:T(1,128)S(1)} all-gather(f32[1,1,512]{2,1,0:T(1,128)S(1)} %bitcast.331), channel_id=6, replica_groups=mesh['tm_0'=8,'tm_1'=4,'tm_2'=2,'blk'=4] {'tm_1'}, dimensions={0}, use_global_device_ids=true | all-gather | bytes 10240 | tf_op jit(solution)/shard_map/all_gather | solution.py:39
  245.1 2.4 fusion.67
  247.6 3.0 fusion.20
  254.6 23.5 %all-gather.14 = f32[8,1,512]{2,1,0:T(1,128)S(1)} all-gather(f32[1,1,512]{2,1,0:T(1,128)S(1)} %bitcast.342), channel_id=7, replica_groups=mesh['tm_0'=8,'tm_1'=4,'tm_2'=2,'blk'=4] {'tm_0'}, dimensions={0}, use_global_device_ids=true | all-gather | bytes 18432 | tf_op jit(solution)/shard_map/all_gather | solution.py:39
  279.2 3.0 fusion.6
  282.1 10.2 %all-gather.38.cloned.1.call-done = f32[4096,512]{1,0:T(8,128)} async-done(((f32[512,512]{1,0:T(8,128)}), f32[4096,512]{1,0:T(8,128)}) %all-gather.38.cloned.1.call-update) | async-done | bytes 8388624 | tf_op jit(solution)/shard_map/all_gather | solution.py:39
  292.3 2.3 fusion.37
  294.6 2.5 fusion.29
  297.2 3.1 fusion.39
  300.3 3.1 fusion.43
  303.3 1.9 fusion.47
  305.2 1.9 fusion.51
  307.1 2.3 fusion.55
  309.3 1.9 fusion.59
  311.2 2.1 convolution_select_fusion
  316.2 70.8 %all-gather.32.cloned.1.call-done = f32[4096,512]{1,0:T(8,128)} async-done(((f32[512,512]{1,0:T(8,128)}), f32[4096,512]{1,0:T(8,128)}) %all-gather.32.cloned.1.call-update) | async-done | bytes 8388624 | tf_op jit(solution)/shard_map/all_gather | solution.py:39
  387.0 2.3 fusion.89
  389.3 2.3 fusion.93
  391.7 2.5 fusion.97
  394.2 2.2 fusion.101
  396.5 2.2 fusion.105
  398.7 2.2 fusion.109
  400.9 2.4 fusion.113
  403.3 2.2 fusion.116
  407.5 1.9 fusion.91
  409.4 1.9 fusion.95
  411.3 1.9 fusion.99
  413.1 1.9 fusion.103
  415.0 1.9 fusion.107
  416.8 2.1 fusion.111
  418.9 2.1 convolution_select_fusion.1
  426.5 9.7 %all_gather.101 = f32[2,512]{1,0:T(2,128)S(1)} all-gather(f32[2,128]{1,0:T(2,128)S(1)} %bitcast.346), channel_id=1, replica_groups=mesh['tm_0'=8,'tm_1'=4,'tm_2'=2,'blk'=4] {'blk'}, dimensions={1}, use_global_device_ids=true | all-gather | bytes 5120 | tf_op jit(solution)/shard_map/all_gather | solution.py:86
  440.0 11.4 %all-gather.16 = f32[4,1,512]{2,1,0:T(1,128)S(1)} all-gather(f32[1,1,512]{2,1,0:T(1,128)S(1)} %bitcast.330), channel_id=12, replica_groups=mesh['tm_0'=8,'tm_1'=4,'tm_2'=2,'blk'=4] {'tm_1'}, dimensions={0}, use_global_device_ids=true | all-gather | bytes 10240 | tf_op jit(solution)/shard_map/all_gather | solution.py:39
  455.5 23.3 %all-gather.17 = f32[8,1,512]{2,1,0:T(1,128)S(1)} all-gather(f32[1,1,512]{2,1,0:T(1,128)S(1)} %bitcast.337), channel_id=13, replica_groups=mesh['tm_0'=8,'tm_1'=4,'tm_2'=2,'blk'=4] {'tm_0'}, dimensions={0}, use_global_device_ids=true | all-gather | bytes 18432 | tf_op jit(solution)/shard_map/all_gather | solution.py:39
  478.8 2.2 fusion.41
  481.0 2.2 fusion.45
  483.2 2.2 fusion.49
  485.4 2.2 fusion.53
  487.7 2.2 fusion.57
  489.9 2.2 fusion.61
  492.1 2.2 fusion.64
  (182 shorter events, 54.5 us)
Async XLA Ops:
  7.2 418.8 %copy-start = (f32[2,128,512]{2,1,0:T(8,128)S(1)}, f32[2,128,512]{2,1,0:T(8,128)}, u32[]{:S(2)}) copy-start(f32[2,128,512]{2,1,0:T(8,128)} %param.11) | copy-start | bytes 1572868
  7.2 47.3 %all-gather.26.cloned.1.call-start = ((), (), s32[]{:S(2)}) async-start(), calls=%async_computation | async-start | bytes 2621440 | tf_op jit(solution)/shard_map/all_gather | solution.py:64
  7.9 64.5 %all-gather.34.cloned.1.call-start = ((), (), s32[]{:S(2)}) async-start(), calls=%async_computation.4 | async-start | bytes 3145728 | tf_op jit(solution)/shard_map/all_gather | solution.py:39
  8.0 15.2 %collective-permute-start = (f32[2,128,512]{2,1,0:T(8,128)}, f32[2,128,512]{2,1,0:T(8,128)S(1)}, u32[]{:S(2)}, u32[]{:S(2)}) collective-permute-start(f32[2,128,512]{2,1,0:T(8,128)} %param.10), channel_id=1, source_target_pairs={{0,1},{1,2},{2,3},{3,0},{4,5},{5,6},{6,7},{7,4},{8,9},{9,10},{10,1... | collective-permute-start | bytes 1572872 | tf_op jit(solution)/shard_map/ppermute | solution.py:18
  9.6 15.3 %collective-permute-start.1 = (f32[2,128,512]{2,1,0:T(8,128)}, f32[2,128,512]{2,1,0:T(8,128)}, u32[]{:S(2)}, u32[]{:S(2)}) collective-permute-start(f32[2,128,512]{2,1,0:T(8,128)} %param.10), channel_id=1, source_target_pairs={{0,3},{1,0},{2,1},{3,2},{4,7},{5,4},{6,5},{7,6},{8,11},{9,8},{10,9... | collective-permute-start | bytes 1572872 | tf_op jit(solution)/shard_map/ppermute | solution.py:21
  23.2 24.8 %collective-permute-start.2 = (f32[2,128,512]{2,1,0:T(8,128)S(1)}, f32[2,128,512]{2,1,0:T(8,128)}, u32[]{:S(2)}, u32[]{:S(2)}) collective-permute-start(f32[2,128,512]{2,1,0:T(8,128)S(1)} %collective-permute-done), channel_id=1, source_target_pairs={{0,1},{1,2},{2,3},{3,0},{4,5},{5,6},{6,7},{7,4},{8,9},{9,10},{10,1... | collective-permute-start | bytes 1572872 | tf_op jit(solution)/shard_map/ppermute | solution.py:18
  51.9 39.5 %all-gather.28.cloned.1.call-start = ((), (), s32[]{:S(2)}) async-start(), calls=%async_computation.1 | async-start | bytes 3145728 | tf_op jit(solution)/shard_map/all_gather | solution.py:39
  58.9 86.3 %all-gather.36.cloned.1.call-start = ((), (), s32[]{:S(2)}) async-start(), calls=%async_computation.5 | async-start | bytes 5242880 | tf_op jit(solution)/shard_map/all_gather | solution.py:39
  74.6 1.0 copy-start.20
  79.7 118.3 %all-gather.30.cloned.1.call-start = ((), (), s32[]{:S(2)}) async-start(), calls=%async_computation.2 | async-start | bytes 5242880 | tf_op jit(solution)/shard_map/all_gather | solution.py:39
  93.6 1.0 copy-start.13
  98.7 193.6 %all-gather.38.cloned.1.call-start = ((), (), s32[]{:S(2)}) async-start(), calls=%async_computation.6 | async-start | bytes 9437184 | tf_op jit(solution)/shard_map/all_gather | solution.py:39
  145.1 7.4 %copy-start.5 = (f32[2048,512]{1,0:T(8,128)S(1)}, f32[2048,512]{1,0:T(8,128)}, u32[]{:S(2)}) copy-start(f32[2048,512]{1,0:T(8,128)} %all-gather.36.cloned.1.call-done) | copy-start | bytes 12582916
  147.5 1.0 copy-start.27
  151.6 1.0 copy-start.16
  154.4 1.0 copy-start.18
  158.3 228.7 %all-gather.32.cloned.1.call-start = ((), (), s32[]{:S(2)}) async-start(), calls=%async_computation.3 | async-start | bytes 9437184 | tf_op jit(solution)/shard_map/all_gather | solution.py:39
  197.9 7.4 %copy-start.7 = (f32[2048,512]{1,0:T(8,128)S(1)}, f32[2048,512]{1,0:T(8,128)}, u32[]{:S(2)}) copy-start(f32[2048,512]{1,0:T(8,128)} %all-gather.30.cloned.1.call-done) | copy-start | bytes 12582916
  200.3 1.0 copy-start.25
  204.4 1.0 copy-start.9
  205.4 5.8 %copy-start.34 = (f32[2,128,128]{2,1,0:T(8,128)S(1)}, f32[2,128,128]{2,1,0:T(8,128)}, u32[]{:S(2)}) copy-start(f32[2,128,128]{2,1,0:T(8,128)} %param.12) | copy-start | bytes 393220
  205.4 5.8 %copy-start.37 = (f32[2,128]{1,0:T(2,128)S(1)}, f32[2,128]{1,0:T(2,128)}, u32[]{:S(2)}) copy-start(f32[2,128]{1,0:T(2,128)} %param.13) | copy-start | bytes 3076
  207.2 1.0 copy-start.11
  211.1 16.0 %copy-start.3 = (f32[2,512,512]{2,1,0:T(8,128)S(1)}, f32[2,512,512]{2,1,0:T(8,128)}, u32[]{:S(2)}) copy-start(f32[2,512,512]{2,1,0:T(8,128)} %all-gather.26.cloned.1.call-done) | copy-start | bytes 6291460
  211.2 20.0 %copy-start.33 = (f32[1024,512]{1,0:T(8,128)S(1)}, f32[1024,512]{1,0:T(8,128)}, u32[]{:S(2)}) copy-start(f32[1024,512]{1,0:T(8,128)} %all-gather.28.cloned.1.call-done) | copy-start | bytes 6291460
  222.3 21.6 %copy-start.14 = (f32[512,512]{1,0:T(8,128)S(1)}, f32[512,512]{1,0:T(8,128)}, u32[]{:S(2)}) copy-start(f32[512,512]{1,0:T(8,128)} %copy-done.13) | copy-start | bytes 3145732
  222.3 21.6 %copy-start.15 = (f32[512,512]{1,0:T(8,128)S(1)}, f32[512,512]{1,0:T(8,128)}, u32[]{:S(2)}) copy-start(f32[512,512]{1,0:T(8,128)} %fusion.136) | copy-start | bytes 3145732
  227.1 20.4 %copy-start.30 = (f32[512,512]{1,0:T(8,128)}, f32[512,512]{1,0:T(8,128)S(1)}, u32[]{:S(2)}) copy-start(f32[512,512]{1,0:T(8,128)S(1)} %fusion.15) | copy-start | bytes 3145732
  227.2 20.4 %copy-start.17 = (f32[512,512]{1,0:T(8,128)S(1)}, f32[512,512]{1,0:T(8,128)}, u32[]{:S(2)}) copy-start(f32[512,512]{1,0:T(8,128)} %copy-done.16) | copy-start | bytes 3145732
  227.2 20.4 %copy-start.19 = (f32[512,512]{1,0:T(8,128)S(1)}, f32[512,512]{1,0:T(8,128)}, u32[]{:S(2)}) copy-start(f32[512,512]{1,0:T(8,128)} %copy-done.18) | copy-start | bytes 3145732
  227.2 20.4 %copy-start.24 = (f32[512,512]{1,0:T(8,128)S(1)}, f32[512,512]{1,0:T(8,128)}, u32[]{:S(2)}) copy-start(f32[512,512]{1,0:T(8,128)} %fusion.77) | copy-start | bytes 3145732
  227.2 20.4 %copy-start.28 = (f32[512,512]{1,0:T(8,128)S(1)}, f32[512,512]{1,0:T(8,128)}, u32[]{:S(2)}) copy-start(f32[512,512]{1,0:T(8,128)} %copy-done.27) | copy-start | bytes 3145732
  245.1 5.4 %copy-start.8 = (f32[2048,512]{1,0:T(8,128)S(1)}, f32[2048,512]{1,0:T(8,128)}, u32[]{:S(2)}) copy-start(f32[2048,512]{1,0:T(8,128)} %all-gather.30.cloned.1.call-done) | copy-start | bytes 12582916
  250.6 28.5 %copy-start.10 = (f32[512,512]{1,0:T(8,128)S(1)}, f32[512,512]{1,0:T(8,128)}, u32[]{:S(2)}) copy-start(f32[512,512]{1,0:T(8,128)} %copy-done.9) | copy-start | bytes 3145732
  250.6 28.6 %copy-start.12 = (f32[512,512]{1,0:T(8,128)S(1)}, f32[512,512]{1,0:T(8,128)}, u32[]{:S(2)}) copy-start(f32[512,512]{1,0:T(8,128)} %copy-done.11) | copy-start | bytes 3145732
  250.6 28.6 %copy-start.23 = (f32[512,512]{1,0:T(8,128)S(1)}, f32[512,512]{1,0:T(8,128)}, u32[]{:S(2)}) copy-start(f32[512,512]{1,0:T(8,128)} %fusion.129) | copy-start | bytes 3145732
  250.6 28.6 %copy-start.26 = (f32[512,512]{1,0:T(8,128)S(1)}, f32[512,512]{1,0:T(8,128)}, u32[]{:S(2)}) copy-start(f32[512,512]{1,0:T(8,128)} %copy-done.25) | copy-start | bytes 3145732
  292.3 11.1 %copy-start.1 = (f32[4096,512]{1,0:T(8,128)S(1)}, f32[4096,512]{1,0:T(8,128)}, u32[]{:S(2)}) copy-start(f32[4096,512]{1,0:T(8,128)} %all-gather.38.cloned.1.call-done) | copy-start | bytes 25165828
  311.2 2.1 copy-start.21
  311.2 4.0 copy-start.35
  387.0 18.5 %copy-start.29 = (f32[512,512]{1,0:T(8,128)S(1)}, f32[512,512]{1,0:T(8,128)}, u32[]{:S(2)}) copy-start(f32[512,512]{1,0:T(8,128)} %fusion.6) | copy-start | bytes 3145732
  389.3 17.2 %copy-start.2 = (f32[4096,512]{1,0:T(8,128)S(1)}, f32[4096,512]{1,0:T(8,128)}, u32[]{:S(2)}) copy-start(f32[4096,512]{1,0:T(8,128)} %all-gather.32.cloned.1.call-done) | copy-start | bytes 25165828
  418.9 4.0 copy-start.36
  418.9 20.1 %copy-start.32 = (f32[1024,512]{1,0:T(8,128)S(1)}, f32[1024,512]{1,0:T(8,128)}, u32[]{:S(2)}) copy-start(f32[1024,512]{1,0:T(8,128)} %all-gather.34.cloned.1.call-done) | copy-start | bytes 6291460
  421.1 2.9 copy-start.4
  421.1 30.4 %copy-start.6 = (f32[2048,512]{1,0:T(8,128)S(1)}, f32[2048,512]{1,0:T(8,128)}, u32[]{:S(2)}) copy-start(f32[2048,512]{1,0:T(8,128)} %all-gather.36.cloned.1.call-done) | copy-start | bytes 12582916
  423.9 30.5 %copy-start.31 = (f32[512,512]{1,0:T(8,128)S(1)}, f32[512,512]{1,0:T(8,128)}, u32[]{:S(2)}) copy-start(f32[512,512]{1,0:T(8,128)} %copy-done.30) | copy-start | bytes 3145732
  454.5 39.9 %copy-start.22 = (f32[512,512]{1,0:T(8,128)S(1)}, f32[512,512]{1,0:T(8,128)}, u32[]{:S(2)}) copy-start(f32[512,512]{1,0:T(8,128)} %fusion.20) | copy-start | bytes 3145732
Sparse Core Ops, SparseCore 0:
  9.8 44.6 all-gather.25
  56.3 16.0 all-gather.33
  74.2 17.1 all-gather.27
  93.1 52.0 all-gather.35
  146.8 51.0 all-gather.29
  199.6 92.6 all-gather.37
  294.1 92.9 all-gather.31
